TPU v7x, 128 devices: a whole 4x4x4 slice. The times are simulated.
128 devices in a mesh: ens: 8 (over x, core), dp: 16 (over y, z).
Axes of the slice: x: 4, y: 4, z: 4, core: 2. Of those that a mesh axis runs over, the one named last changes fastest.
Arguments:
- features: bfloat16 [6144, 256], P('dp'), may hold values from -4 to 4
- reward: float32 [6144], P('dp'), may hold values from -16 to 16
- done: int32 [6144], P('dp'), may hold values 0 or 1
- value_next: float32 [6144], P('dp'), may hold values from -16 to 16
- value_now: float32 [6144], P('dp'), may hold values from -4 to 4
- w_in: bfloat16 [16, 256, 2048], P('ens'), may hold values from -0.375 to 0.375
- w_mid: bfloat16 [16, 2048, 2048], P('ens'), may hold values from -0.099121094 to 0.099121094
- biases: float32 [2, 16, 2048], P(None, 'ens'), may hold values from -3 to 3
- w_out: bfloat16 [16, 2048], P('ens'), may hold values from -0.011048543 to 0.011048543
Outputs:
- value_grad: float32 [6144], P('dp')
- d_in: float32 [256, 16, 2048], P('dp', 'ens')
- d_mid: float32 [2048, 16, 2048], P('dp', 'ens')
- d_bias: float32 [2, 16, 2048], P(None, 'ens', 'dp')
- d_out: float32 [16, 2048], P('ens', 'dp')
All inputs are finite; a program needn't handle non-finite values. No bound on the sum of `done` on one device may be relied on, other than what follows from the above.
Results may differ from a plain program's by a relative error of at most 0.013.
Values may be sent and summed in bfloat16 or wider, within the bound.
A program may use at most 128 MiB of HBM per device.

v0:
```python
import jax
import jax.numpy as jnp
from jax import lax
from jax.sharding import PartitionSpec as P


def sent_to_all(value, axis):
    copies = jnp.broadcast_to(value, (lax.axis_size(axis), *value.shape))
    return lax.all_to_all(copies, axis, split_axis=0, concat_axis=0, tiled=True)


def of_everyone(value, axis):
    return sent_to_all(value, axis).min(axis=0)


def split_up(value, dim, length):
    dims = value.shape
    pieces = value.reshape(*dims[:dim], length, dims[dim] // length, *dims[dim + 1 :])
    return jnp.moveaxis(pieces, dim, 0)


def one_scatter(arrays, axis, dims):
    length = lax.axis_size(axis)
    pieces = [split_up(a, dim, length) for a, dim in zip(arrays, dims)]
    lines = jnp.concatenate([b.reshape(length, -1) for b in pieces], axis=1)
    span = max(16, -(-lines.shape[1] // 1024) * 8)
    lines = jnp.pad(lines, ((0, 0), (0, span * 128 - lines.shape[1]))).reshape(-1, 128)
    ravelled, at, outs = (lax.psum_scatter(lines, axis, tiled=True).reshape(-1), 0, [])
    for b in pieces:
        part = b[0]
        outs.append(ravelled[at : at + part.size].reshape(part.shape))
        at += part.size
    return tuple(outs)


def silu_slope(value):
    sig = jax.nn.sigmoid(value)
    return sig * (1.0 + value * (1.0 - sig))


def per_device(features, reward, done, value_next, value_now, w_in, w_mid, biases, w_out):
    pre_one = (
        jnp.einsum("ra,hak->hrk", features, w_in, preferred_element_type=jnp.float32)
        + biases[0][:, None, :]
    )
    act_one = jax.nn.silu(pre_one).astype(jnp.bfloat16)
    pre_two = (
        jnp.einsum("hrk,hkj->hrj", act_one, w_mid, preferred_element_type=jnp.float32)
        + biases[1][:, None, :]
    )
    act_two = jax.nn.silu(pre_two).astype(jnp.bfloat16)
    q_values = jnp.einsum("hrj,hj->hr", act_two, w_out, preferred_element_type=jnp.float32)
    q_min = of_everyone(jnp.min(q_values, axis=0), "ens")
    gap = q_min - value_now
    weight = jnp.where(gap < 0.0, 0.3, 0.7)
    value_grad = -2.0 * weight * gap
    target = reward + 0.99 * (1.0 - done.astype(jnp.float32)) * value_next
    error = q_values - target[None, :]
    delta_two = (
        error[:, :, None] * w_out.astype(jnp.float32)[:, None, :] * silu_slope(pre_two)
    ).astype(jnp.bfloat16)
    grad_out = jnp.einsum("hr,hrj->hj", error, act_two, preferred_element_type=jnp.float32)
    grad_two = jnp.sum(delta_two.astype(jnp.float32), axis=1)
    d_mid = lax.psum_scatter(
        jnp.einsum("hrk,hrj->khj", act_one, delta_two, preferred_element_type=jnp.float32).astype(
            jnp.bfloat16
        ),
        "dp",
        scatter_dimension=0,
        tiled=True,
    ).astype(jnp.float32)
    back = jnp.einsum("hrj,hkj->hrk", delta_two, w_mid, preferred_element_type=jnp.float32)
    delta_one = (back * silu_slope(pre_one)).astype(jnp.bfloat16)
    grad_in = jnp.einsum("ra,hrk->ahk", features, delta_one, preferred_element_type=jnp.float32)
    grad_one = jnp.sum(delta_one.astype(jnp.float32), axis=1)
    grad_in, grad_bias = (grad_in, jnp.stack([grad_one, grad_two]))
    d_in, d_bias, d_out = tuple(
        (
            part.astype(jnp.float32)
            for part in one_scatter(
                (
                    grad_in.astype(jnp.bfloat16),
                    grad_bias.astype(jnp.bfloat16),
                    grad_out.astype(jnp.bfloat16),
                ),
                "dp",
                (0, 2, 1),
            )
        )
    )
    return (value_grad, d_in, d_mid, d_bias, d_out)


def solution(mesh):
    in_specs = (
        P("dp", None),
        P("dp"),
        P("dp"),
        P("dp"),
        P("dp"),
        P("ens", None, None),
        P("ens", None, None),
        P(None, "ens", None),
        P("ens", None),
    )
    out_specs = (
        P("dp"),
        P("dp", "ens", None),
        P("dp", "ens", None),
        P(None, "ens", "dp"),
        P("ens", "dp"),
    )
    return jax.shard_map(
        per_device, mesh=mesh, in_specs=in_specs, out_specs=out_specs, check_vma=False
    )
```

profile of v0, /device:TPU:1, one launch (start us, length us, event | category | flops | bytes accessed | tf_op | source)
XLA Modules:
  0.0 278.2 jit_solution(13899473329896805526)
XLA Ops:
  7.2 0.0 copy-start
  7.2 0.0 all-reduce.4.cloned.1.call-start
  7.2 1.4 convert_element_type.64
  8.7 1.3 slice_bitcast_fusion
  10.0 0.0 copy-done
  10.0 1.9 fusion.15
  11.9 0.0 copy-start.2
  11.9 0.0 copy-start.4
  12.0 0.0 copy-start.9
  12.0 0.0 copy-start.10
  12.0 0.0 copy-start.11
  12.0 13.4 %multiply_convert_fusion.1 = (bf16[2,384,2048]{2,1,0:T(8,128)(2,1)S(1)}, f32[2,384,2048]{2,1,0:T(8,128)S(1)}) fusion(f32[2,2048]{1,0:T(2,128)} %get-tuple-element.32, bf16[2,2048,2048]{2,1,0:T(8,128)(2,1)} %param.15, f32[2,2048,384]{1,2,0:T(8,128)S(1)} %fusion.15, f32[2,2048]{1,0:T(2,128)} %get-tuple-element.33), kind=kOutput, calls=%fused_computation.13 | convolution fusion | flops 6461325312 | bytes 32538624 | tf_op jit(solution)/shard_map/hrk,hkj->hrj/dot_general | solution.py:48
  25.4 0.0 copy-done.2
  25.4 0.0 copy-start.5
  25.4 0.0 copy-start.6
  25.4 0.0 copy-done.4
  25.4 0.9 fusion.17
  26.3 0.0 copy-done.9
  26.3 0.0 copy-done.10
  26.4 0.0 copy-done.11
  26.4 0.0 copy-start.7
  26.4 0.5 fusion.19
  27.0 0.0 copy-done.5
  27.0 0.0 copy-done.6
  27.0 4.0 %fusion.25 = (bf16[2,2048]{1,0:T(2,128)(2,1)S(1)}, bf16[2,384,2048]{2,1,0:T(8,128)(2,1)}) fusion(f32[2,384,2048]{2,1,0:T(8,128)S(1)} %get-tuple-element.37, f32[2,2048]{1,0:T(2,128)S(1)} %copy-done.6, f32[2,2048]{1,0:T(2,128)S(1)} %copy-done.5, f32[2,384]{1,0:T(2,128)S(1)} %get-tuple-element.34), kind=kLoop, calls=%fused_computation.44 | loop fusion | flops 18870272 | bytes 9481216 | tf_op jit(solution)/shard_map/reduce_sum | solution.py:63
  31.0 0.0 copy-done.7
  31.0 0.0 copy-start.3
  31.0 14.6 %fusion.26 = (bf16[2,2048]{1,0:T(2,128)(2,1)S(1)}, bf16[2,384,2048]{2,1,0:T(8,128)(2,1)}) fusion(f32[2,2048,384]{1,2,0:T(8,128)} %copy-done.2, f32[2,2048]{1,0:T(2,128)S(1)} %copy-done.7, bf16[2,384,2048]{2,1,0:T(8,128)(2,1)} %get-tuple-element.31, bf16[2,2048,2048]{2,1,0:T(8,128)(2,1)} %param.15), kind=kOutput, calls=%fused_computation.45 | convolution fusion | flops 6459748352 | bytes 29384704 | tf_op jit(solution)/shard_map/hrj,hkj->hrk/dot_general | solution.py:72
  45.7 0.0 copy-done.3
  45.7 3.2 %fusion.11 = bf16[256,2,2048]{0,2,1:T(8,128)(2,1)S(1)} fusion(bf16[2,384,2048]{2,1,0:T(8,128)(2,1)} %get-tuple-element.39, bf16[384,256]{1,0:T(8,128)(2,1)S(1)} %copy-done.3), kind=kOutput, calls=%fused_computation.20 | convolution fusion | flops 806354944 | bytes 5439488 | tf_op jit(solution)/shard_map/ra,hrk->ahk/dot_general | solution.py:74
  48.9 3.9 %copy.31 = bf16[256,2,2048]{2,1,0:T(2,128)(2,1)} copy(bf16[256,2,2048]{0,2,1:T(8,128)(2,1)S(1)} %fusion.11) | data formatting | bytes 4194304 | tf_op jit(solution)/shard_map/convert_element_type | solution.py:82
  52.9 2.9 %reshape_reshape.3 = bf16[16,65536]{1,0:T(8,128)(2,1)S(1)} reshape(bf16[256,2,2048]{2,1,0:T(2,128)(2,1)} %copy.31) | data formatting | bytes 4194304 | tf_op jit(solution)/shard_map/reshape;reshape | solution.py:25
  55.8 1.5 fusion.13
  57.2 3.2 %reshape.55 = bf16[8320,128]{1,0:T(8,128)(2,1)} reshape(bf16[16,66560]{1,0:T(8,128)(2,1)} %fusion.13) | data formatting | bytes 4259840 | tf_op jit(solution)/shard_map/reshape | solution.py:27
  60.4 0.0 all-reduce.4.cloned.1.call-update
  60.5 0.0 reduce-scatter.4.cloned.1.call-start
  60.5 15.8 %convolution_convert_fusion = bf16[2,2048,2048]{2,1,0:T(8,128)(2,1)} fusion(bf16[2,384,2048]{2,1,0:T(8,128)(2,1)} %get-tuple-element.31, f32[2,2048,384]{1,2,0:T(8,128)} %copy-done.2, f32[2,2048]{1,0:T(2,128)S(1)} %copy-done.7), kind=kOutput, calls=%fused_computation | convolution fusion | flops 6460276736 | bytes 26230784 | tf_op jit(solution)/shard_map/hrk,hrj->khj/dot_general | solution.py:65
  76.3 21.3 %copy.42 = bf16[2048,4096]{1,0:T(8,128)(2,1)} copy(bf16[2048,4096]{0,1:T(8,128)(2,1)} %bitcast.74) | data formatting | bytes 33554432
  97.6 0.0 copy-start.12
  97.6 0.0 copy-start.8
  97.6 0.0 reduce-scatter.4.cloned.1.call-update
  97.6 0.0 copy-start.1
  97.6 0.6 broadcast_in_dim.14
  98.3 6.1 %all-to-all-start = ((f32[8,1,384]{2,1,0:T(1,128)}), f32[8,1,384]{2,1,0:T(1,128)S(1)}, u32[]{:S(2)}, u32[]{:S(2)}) async-start(f32[8,1,384]{2,1,0:T(1,128)} %broadcast_in_dim.14), calls=%async_computation | async-start | bytes 24576 | tf_op jit(solution)/shard_map/all_to_all | solution.py:9
  104.3 0.0 copy-done.12
  104.3 0.6 dynamic-slice
  105.6 3.4 %all-to-all-done = f32[8,1,384]{2,1,0:T(1,128)S(1)} async-done(((f32[8,1,384]{2,1,0:T(1,128)}), f32[8,1,384]{2,1,0:T(1,128)S(1)}, u32[]{:S(2)}, u32[]{:S(2)}) %all-to-all-start) | async-done | bytes 12320 | tf_op jit(solution)/shard_map/all_to_all | solution.py:9
  109.0 0.0 copy-done.8
  109.0 0.6 multiply_multiply_fusion
  109.6 43.7 %all-reduce.4.cloned.1.call-done = bf16[8320,128]{1,0:T(8,128)(2,1)} async-done(((bf16[8320,128]{1,0:T(8,128)(2,1)}), bf16[8320,128]{1,0:T(8,128)(2,1)}) %all-reduce.4.cloned.1.call-update) | async-done | bytes 2129936
  153.3 0.9 dynamic-slice_convert_fusion
  154.2 0.8 reshape.56
  155.0 0.7 constant_dynamic-slice_fusion
  155.7 0.6 convert.14
  156.3 1.2 fusion.21
  157.5 110.1 %reduce-scatter.4.cloned.1.call-done = bf16[128,4096]{1,0:T(8,128)(2,1)} async-done(((bf16[2048,4096]{1,0:T(8,128)(2,1)}), bf16[128,4096]{1,0:T(8,128)(2,1)}) %reduce-scatter.4.cloned.1.call-update) | async-done | bytes 1048592
  267.7 1.6 copy.43
  269.3 2.1 copy.33
  271.4 0.0 copy-done.1
  (7 shorter events, 0.1 us)
Async XLA Ops:
  7.2 2.9 %copy-start = (bf16[2,256,2048]{2,1,0:T(8,128)(2,1)S(1)}, bf16[2,256,2048]{2,1,0:T(8,128)(2,1)}, u32[]{:S(2)}) copy-start(bf16[2,256,2048]{2,1,0:T(8,128)(2,1)} %param.14) | copy-start | bytes 6291460
  7.2 146.1 %all-reduce.4.cloned.1.call-start = ((), (), s32[]{:S(2)}) async-start(), calls=%async_computation.3 | async-start | bytes 4259840
  11.9 13.5 %copy-start.2 = (f32[2,2048,384]{1,2,0:T(8,128)}, f32[2,2048,384]{1,2,0:T(8,128)S(1)}, u32[]{:S(2)}) copy-start(f32[2,2048,384]{1,2,0:T(8,128)S(1)} %fusion.15) | copy-start | bytes 18874372
  11.9 13.5 %copy-start.4 = (bf16[2,2048]{1,0:T(2,128)(2,1)S(1)}, bf16[2,2048]{1,0:T(2,128)(2,1)}, u32[]{:S(2)}) copy-start(bf16[2,2048]{1,0:T(2,128)(2,1)} %param.17) | copy-start | bytes 24580
  12.0 14.4 %copy-start.9 = (f32[384]{0:T(512)S(1)}, f32[384]{0:T(512)}, u32[]{:S(2)}) copy-start(f32[384]{0:T(512)} %param.10) | copy-start | bytes 4612
  12.0 14.4 %copy-start.10 = (f32[384]{0:T(512)S(1)}, f32[384]{0:T(512)}, u32[]{:S(2)}) copy-start(f32[384]{0:T(512)} %param.12) | copy-start | bytes 4612
  12.0 14.4 %copy-start.11 = (s32[384]{0:T(512)S(1)}, s32[384]{0:T(512)}, u32[]{:S(2)}) copy-start(s32[384]{0:T(512)} %param.11) | copy-start | bytes 4612
  25.4 1.6 copy-start.5
  25.4 1.6 copy-start.6
  26.4 4.6 %copy-start.7 = (f32[2,2048]{1,0:T(2,128)S(1)}, f32[2,2048]{1,0:T(2,128)}, u32[]{:S(2)}) copy-start(f32[2,2048]{1,0:T(2,128)} %get-tuple-element.33) | copy-start | bytes 49156
  31.0 14.7 %copy-start.3 = (bf16[384,256]{1,0:T(8,128)(2,1)S(1)}, bf16[384,256]{1,0:T(8,128)(2,1)}, u32[]{:S(2)}) copy-start(bf16[384,256]{1,0:T(8,128)(2,1)} %param.9) | copy-start | bytes 589828
  60.5 207.2 %reduce-scatter.4.cloned.1.call-start = ((), (), s32[]{:S(2)}) async-start(), calls=%async_computation.2 | async-start | bytes 17825792
  97.6 6.7 %copy-start.12 = (u32[128]{0:T(128)S(1)}, u32[128]{0:T(128)}, u32[]{:S(2)}) copy-start(u32[128]{0:T(128)} %constant.32) | copy-start | bytes 1540
  97.6 11.4 %copy-start.8 = (f32[384]{0:T(512)S(1)}, f32[384]{0:T(512)}, u32[]{:S(2)}) copy-start(f32[384]{0:T(512)} %param.13) | copy-start | bytes 4612
  97.6 173.8 %copy-start.1 = (bf16[2,256,2048]{2,1,0:T(8,128)(2,1)S(1)}, bf16[2,256,2048]{2,1,0:T(8,128)(2,1)}, u32[]{:S(2)}) copy-start(bf16[2,256,2048]{2,1,0:T(8,128)(2,1)} %param.14) | copy-start | bytes 6291460
  98.3 10.7 %all-to-all-start = ((f32[8,1,384]{2,1,0:T(1,128)}), f32[8,1,384]{2,1,0:T(1,128)S(1)}, u32[]{:S(2)}, u32[]{:S(2)}) async-start(f32[8,1,384]{2,1,0:T(1,128)} %broadcast_in_dim.14), calls=%async_computation | async-start | bytes 24576 | tf_op jit(solution)/shard_map/all_to_all | solution.py:9
Sparse Core Ops, SparseCore 0:
  60.6 92.6 all-reduce.3
  156.7 110.9 reduce-scatter.3
where the time goes:
time: 279 us; the launch traced here: 278 us
  waiting for transfers between devices  157 us (56%)
  matrix products  50.3 us (18%)
  local copies, waits for them, and re-layouts  39.3 us (14%)
  between operations  14.9 us (5%)
  other arithmetic  10.4 us (4%)
  starting transfers between devices  6.15 us (2%)
    unnamed x4, waiting for transfers between devices  154 us
    unnamed x31, local copies, waits for them, and re-layouts  25.7 us
    dot_general x1, matrix products, per_device(): jnp.einsum('hrk,hrj->khj', act_one, delta_two, preferred_element_type=jnp...  15.8 us
    dot_general x1, matrix products, per_device(): jnp.einsum('hrj,hkj->hrk', delta_two, w_mid, preferred_element_type=jnp.f...  14.6 us
    dot_general x1, matrix products, per_device(): jnp.einsum('hrk,hkj->hrj', act_one, w_mid, preferred_element_type=jnp.flo...  13.4 us
    all_to_all x1, starting transfers between devices, sent_to_all(): return lax.all_to_all(copies, axis, split_axis=0, concat_axis=0, tiled=True)  6.07 us
  transfers between devices with their start and end apart: 3, of which 3 were waited for; matrix products, arithmetic and copies ran while one was open for 16% of the time, Pallas kernels for 0%

commit v1 on v0

v1 whole, which is shorter than its diff:
```python
import jax
import jax.numpy as jnp
from jax import lax
from jax.experimental import pallas as pl
from jax.experimental.pallas import tpu as pltpu
from jax.sharding import PartitionSpec as P

MESH = pl.DeviceIdType.MESH
BF = jnp.bfloat16
F32 = jnp.float32
ROWS = 384
IN = 256
H = 2048
R2 = 2 * ROWS
C = 256
NC = H // C
GW = H + 256
HALF = H // 2
GH = GW // 2


def tn(a, b, **kw):
    return lax.dot_general(a, b, (((1,), (0,)), ((), ())), preferred_element_type=F32, **kw)


def nt(a, b, **kw):
    return lax.dot_general(a, b, (((1,), (1,)), ((), ())), preferred_element_type=F32, **kw)


def chunk(n, width=C):
    return pl.ds(pl.multiple_of(n * width, width), width)


def kernel(
    feat_hbm, reward, done, vnext, vnow, win_hbm, wmid_hbm, biases, wout,
    vg_out, mid_out, gin_out,
    feat, win, wmid, act1, sl1, act2, sl2, del2, accq, eb, stats, part, lhs, featT,
    r1a, r1b, r2a, r2b, r3, gp, g1a, g1b, g2a, g2b, g3,
    tgt, tgtm, qm, qr, mo, ms, mm, mx,
    lsem, wsem, osem, ssem, rsem,
):
    ens = lax.axis_index("ens")
    dp = lax.axis_index("dp")
    core = lax.rem(ens, 2)
    xpos = lax.div(ens, 2)
    y = lax.div(dp, 4)
    z = lax.rem(dp, 4)
    u = jnp.where(core == 0, y, z)
    v = jnp.where(core == 0, z, y)
    su = 4 - 3 * core
    sv = 1 + 3 * core
    head = lax.div(v, 2)

    def dp_of(ru, rv):
        return (u ^ ru) * su + (v ^ rv) * sv

    def dev(ru, rv):
        return (ens, dp_of(ru, rv))

    u1, u3, v1, v3 = dev(1, 0), dev(3, 0), dev(0, 1), dev(0, 3)
    sib = (ens ^ 1, dp)
    xs = [((xpos ^ k) * 2 + core, dp) for k in (1, 2, 3)]

    loads = [
        pltpu.make_async_copy(feat_hbm, feat.at[pl.ds(0, ROWS)], lsem.at[0]),
        pltpu.make_async_copy(win_hbm.at[head], win, lsem.at[1]),
    ]
    for n in range(NC):
        loads.append(
            pltpu.make_async_copy(
                wmid_hbm.at[head, :, pl.ds(n * C, C)], wmid.at[:, pl.ds(n * C, C)], wsem.at[n]
            )
        )
    for copy in loads:
        copy.start()

    barrier = pltpu.get_barrier_semaphore()
    partners = [u1, u3, v1, v3, sib, *xs]
    for p in partners:
        pl.semaphore_signal(barrier, inc=1, device_id=p, device_id_type=MESH)

    target = reward[...] + 0.99 * (1.0 - done[...].astype(F32)) * vnext[...]
    tgt[...] = jnp.broadcast_to(target, (8, ROWS))
    pl.semaphore_wait(barrier, len(partners))

    copies = []

    def send(src, dst, to):
        i = len(copies)
        copy = pltpu.make_async_remote_copy(
            src_ref=src, dst_ref=dst, send_sem=ssem.at[i], recv_sem=rsem.at[i],
            device_id=to, device_id_type=MESH,
        )
        copies.append(copy)
        copy.start()
        return copy

    loads[0].wait()
    got_feat = send(feat.at[pl.ds(0, ROWS)], feat.at[pl.ds(ROWS, ROWS)], v3)
    got_tgt = send(tgt, tgtm, v3)
    loads[1].wait()

    wo = wout[...].astype(F32)
    wo = jnp.where(head == 0, wo[0:1], wo[1:2])
    b_all = biases[...]
    b_one = jnp.where(head == 0, b_all[0, 0:1], b_all[0, 1:2])
    b_two = jnp.where(head == 0, b_all[1, 0:1], b_all[1, 1:2])
    stats[...] = jnp.zeros_like(stats)
    stats[0:1, :] = b_one
    stats[1:2, :] = b_two
    stats[2:3, :] = wo

    def silu_both(val):
        s = 0.5 * jnp.tanh(0.5 * val) + 0.5
        act = val * s
        return act, s + act * (1.0 - s)

    for p in range(2):
        rows = pl.ds(p * ROWS, ROWS)
        if p == 1:
            got_feat.wait_recv()

        @pl.loop(0, NC)
        def _(n):
            cols = chunk(n)
            val = tn(feat[rows, :], win[:, cols]) + stats[0:1, cols]
            act, slope = silu_both(val)
            act1[rows, cols] = act.astype(BF)
            sl1[rows, cols] = slope.astype(BF)

        accq[rows, :] = jnp.zeros((ROWS, 128), F32)
        if p == 0:
            for copy in loads[2:]:
                copy.wait()

        @pl.loop(0, NC)
        def _(n):
            cols = chunk(n)
            val = tn(act1[rows, :], wmid[:, cols]) + stats[1:2, cols]
            act, slope = silu_both(val)
            wrow = stats[2:3, cols]
            prod = act * wrow
            accq[rows, :] += prod[:, :128] + prod[:, 128:]
            act2[rows, cols] = act.astype(BF)
            sl2[rows, cols] = (slope * wrow).astype(BF)

    q = nt(jnp.ones((8, 128), F32), accq[...], precision=lax.Precision.HIGHEST)
    got_tgt.wait_recv()
    qm[...] = q[:, ROWS:]
    mo[...] = q[:, :ROWS]
    got_q = send(qm, qr, v3)
    err = q - jnp.concatenate([tgt[...], tgtm[...]], axis=1)
    eb[...] = jnp.transpose(jnp.broadcast_to(err[0:1], (128, R2)))
    stats[...] = jnp.zeros_like(stats)

    @pl.loop(0, NC)
    def _(n):
        cols = chunk(n)
        e = jnp.concatenate([eb[...], eb[...]], axis=1)
        d = e * sl2[:, cols].astype(F32)
        del2[:, cols] = d.astype(BF)
        stats[1:2, cols] = jnp.sum(d, axis=0, keepdims=True)
        stats[2:3, cols] = jnp.sum(e * act2[:, cols].astype(F32), axis=0, keepdims=True)

    order = (2, 1, 3, 0)

    def group(ru):
        for rv in range(4):
            lhs[pl.ds(rv * 128, 128), :] = jnp.transpose(act1[:, chunk(dp_of(ru, rv), 128)])

    def products(ru, half):
        @pl.loop(half * NC // 2, (half + 1) * NC // 2)
        def _(n):
            cols = chunk(n)
            res = tn(lhs[...], del2[:, cols]).astype(BF)
            for rv in range(4):
                part[ru, rv, :, cols] = res[rv * 128 : (rv + 1) * 128]

    left, right = pl.ds(0, HALF), pl.ds(HALF, HALF)
    one_a, one_b, two_a, two_b = [None] * 4, [None] * 4, [None] * 4, [None] * 4
    group(2)
    products(2, 0)
    for rv in order:
        one_a[rv] = send(part.at[2, rv, :, left], r1a.at[rv], u1)
    products(2, 1)
    for rv in order:
        one_b[rv] = send(part.at[2, rv, :, right], r1b.at[rv], u3)
    group(1)
    products(1, 0)
    for rv in order:
        two_a[rv] = [send(part.at[1, rv, :, left], r2a.at[rv, :, left], u1)]
    products(1, 1)
    group(3)
    products(3, 1)
    for rv in order:
        two_b[rv] = [send(part.at[3, rv, :, right], r2b.at[rv, :, right], u3)]
    products(3, 0)
    group(0)
    products(0, 0)
    products(0, 1)

    got_q.wait_recv()
    mo[...] = jnp.minimum(mo[...], qr[...])
    got_sib = send(mo, ms, sib)

    def merge():
        for rv in order:
            one_a[rv].wait_recv()
            part[3, rv, :, left] = (part[3, rv, :, left].astype(F32) + r1a[rv].astype(F32)).astype(BF)
            two_b[rv].append(send(part.at[3, rv, :, left], r2b.at[rv, :, left], u3))
            one_b[rv].wait_recv()
            part[1, rv, :, right] = (part[1, rv, :, right].astype(F32) + r1b[rv].astype(F32)).astype(BF)
            two_a[rv].append(send(part.at[1, rv, :, right], r2a.at[rv, :, right], u1))

    featT[...] = jnp.transpose(feat[...])

    @pl.loop(0, NC)
    def _(n):
        cols = chunk(n)
        back = nt(del2[...], wmid[cols, :])
        d = back * sl1[:, cols].astype(F32)
        stats[0:1, cols] = jnp.sum(d, axis=0, keepdims=True)
        res = tn(featT[...], d.astype(BF)).astype(BF)
        for i in range(16):
            slot = jnp.where(core == 0, (i // 4 ^ y) * 4 + (i % 4 ^ z), (i % 4 ^ z) * 4 + (i // 4 ^ y))
            gp[slot, :, cols] = res[i * 16 : (i + 1) * 16]

    for i in range(16):
        slot = jnp.where(core == 0, (i // 4 ^ y) * 4 + (i % 4 ^ z), (i % 4 ^ z) * 4 + (i // 4 ^ y))
        tile = jnp.concatenate([stats[:, i * 128 : (i + 1) * 128], jnp.zeros((8, 128), F32)], axis=0)
        gp[slot, :, pl.ds(H, 128)] = tile.astype(BF)
        gp[slot, :, pl.ds(H + 128, 128)] = jnp.zeros((16, 128), BF)

    got_sib.wait_recv()
    mm[...] = jnp.minimum(mo[...], ms[...])
    got_x = [send(mm, mx.at[k], xs[k]) for k in range(3)]

    gl, gr = pl.ds(0, GH), pl.ds(GH, GH)
    g_one_a = send(gp.at[pl.ds(8, 4), :, gl], g1a, u1)
    g_one_b = send(gp.at[pl.ds(8, 4), :, gr], g1b, u3)
    g_two_a = [send(gp.at[pl.ds(4, 4), :, gl], g2a.at[:, :, gl], u1)]
    g_two_b = [send(gp.at[pl.ds(12, 4), :, gr], g2b.at[:, :, gr], u3)]

    merge()

    g_one_a.wait_recv()
    gp[12:16, :, gl] = (gp[12:16, :, gl].astype(F32) + g1a[...].astype(F32)).astype(BF)
    g_two_b.append(send(gp.at[pl.ds(12, 4), :, gl], g2b.at[:, :, gl], u3))
    g_one_b.wait_recv()
    gp[4:8, :, gr] = (gp[4:8, :, gr].astype(F32) + g1b[...].astype(F32)).astype(BF)
    g_two_a.append(send(gp.at[pl.ds(4, 4), :, gr], g2a.at[:, :, gr], u1))

    def ring_sum(rv):
        for copy in (*two_a[rv], *two_b[rv]):
            copy.wait_recv()
        part[0, rv] = (part[0, rv].astype(F32) + r2a[rv].astype(F32) + r2b[rv].astype(F32)).astype(BF)

    ring_sum(2)
    three_3 = send(part.at[0, 2], r3.at[1], v1)
    ring_sum(1)
    three_0 = send(part.at[0, 1], r3.at[0], v1)
    ring_sum(3)
    three_3.wait_recv()
    part[0, 3] = (part[0, 3].astype(F32) + r3[1].astype(F32)).astype(BF)
    four = send(part.at[0, 3], mid_out.at[head], v3)

    for copy in (*g_two_a, *g_two_b):
        copy.wait_recv()
    gp[0:4] = (gp[0:4].astype(F32) + g2a[...].astype(F32) + g2b[...].astype(F32)).astype(BF)
    g_three = send(gp.at[pl.ds(1, 2)], g3, v1)

    ring_sum(0)
    three_0.wait_recv()
    part[0, 0] = (part[0, 0].astype(F32) + r3[0].astype(F32)).astype(BF)
    own_mid = pltpu.make_async_copy(part.at[0, 0], mid_out.at[head], osem.at[0])
    own_mid.start()

    g_three.wait_recv()
    gp[3] = (gp[3].astype(F32) + g3[1].astype(F32)).astype(BF)
    g_four = send(gp.at[3], gin_out.at[head], v3)
    gp[0] = (gp[0].astype(F32) + g3[0].astype(F32)).astype(BF)
    own_gin = pltpu.make_async_copy(gp.at[0], gin_out.at[head], osem.at[1])
    own_gin.start()

    for copy in got_x:
        copy.wait_recv()
    q_min = jnp.minimum(jnp.minimum(mm[...], mx[0]), jnp.minimum(mx[1], mx[2]))
    gap = q_min[0:1] - vnow[...]
    vg_out[...] = -2.0 * jnp.where(gap < 0.0, 0.3, 0.7) * gap

    own_mid.wait()
    own_gin.wait()
    four.wait_recv()
    g_four.wait_recv()
    for copy in copies:
        copy.wait_send()


def per_device(features, reward, done, value_next, value_now, w_in, w_mid, biases, w_out):
    vm = pl.BlockSpec(memory_space=pltpu.VMEM)
    hbm = pl.BlockSpec(memory_space=pl.ANY)
    line = (1, ROWS)
    vg, mid, gin = pl.pallas_call(
        kernel,
        out_shape=(
            jax.ShapeDtypeStruct(line, F32),
            jax.ShapeDtypeStruct((2, 128, H), BF),
            jax.ShapeDtypeStruct((2, 16, GW), BF),
        ),
        in_specs=[hbm, vm, vm, vm, vm, hbm, hbm, vm, vm],
        out_specs=(vm, hbm, hbm),
        scratch_shapes=[
            pltpu.VMEM((R2, IN), BF),
            pltpu.VMEM((IN, H), BF),
            pltpu.VMEM((H, H), BF),
            pltpu.VMEM((R2, H), BF),
            pltpu.VMEM((R2, H), BF),
            pltpu.VMEM((R2, H), BF),
            pltpu.VMEM((R2, H), BF),
            pltpu.VMEM((R2, H), BF),
            pltpu.VMEM((R2, 128), F32),
            pltpu.VMEM((R2, 128), F32),
            pltpu.VMEM((8, H), F32),
            pltpu.VMEM((4, 4, 128, H), BF),
            pltpu.VMEM((512, R2), BF),
            pltpu.VMEM((IN, R2), BF),
            pltpu.VMEM((4, 128, HALF), BF),
            pltpu.VMEM((4, 128, HALF), BF),
            pltpu.VMEM((4, 128, H), BF),
            pltpu.VMEM((4, 128, H), BF),
            pltpu.VMEM((2, 128, H), BF),
            pltpu.VMEM((16, 16, GW), BF),
            pltpu.VMEM((4, 16, GH), BF),
            pltpu.VMEM((4, 16, GH), BF),
            pltpu.VMEM((4, 16, GW), BF),
            pltpu.VMEM((4, 16, GW), BF),
            pltpu.VMEM((2, 16, GW), BF),
            *[pltpu.VMEM((8, ROWS), F32)] * 7,
            pltpu.VMEM((3, 8, ROWS), F32),
            pltpu.SemaphoreType.DMA((2,)),
            pltpu.SemaphoreType.DMA((NC,)),
            pltpu.SemaphoreType.DMA((2,)),
            pltpu.SemaphoreType.DMA((48,)),
            pltpu.SemaphoreType.DMA((48,)),
        ],
        compiler_params=pltpu.CompilerParams(
            collective_id=0, has_side_effects=True, vmem_limit_bytes=67_000_000
        ),
    )(
        features, reward.reshape(line), done.reshape(line), value_next.reshape(line),
        value_now.reshape(line), w_in, w_mid, biases, w_out,
    )
    d_mid = jnp.transpose(mid, (1, 0, 2)).astype(F32)
    d_in = jnp.transpose(gin[:, :, :H], (1, 0, 2)).astype(F32)
    rest = gin[:, :3, H : H + 128].astype(F32)
    d_bias = jnp.transpose(rest[:, :2], (1, 0, 2))
    return vg.reshape(ROWS), d_in, d_mid, d_bias, rest[:, 2]


def solution(mesh):
    in_specs = (
        P("dp", None), P("dp"), P("dp"), P("dp"), P("dp"),
        P("ens", None, None), P("ens", None, None), P(None, "ens", None), P("ens", None),
    )
    out_specs = (
        P("dp"), P("dp", "ens", None), P("dp", "ens", None), P(None, "ens", "dp"), P("ens", "dp"),
    )
    return jax.shard_map(
        per_device, mesh=mesh, in_specs=in_specs, out_specs=out_specs, check_vma=False
    )
```

time: 279 us -> 100 us (0.36)
  waiting for transfers between devices: 157 us -> 0 us
  Pallas kernels: 0 us -> 85.7 us
  matrix products: 50.3 us -> 0 us
  local copies, waits for them, and re-layouts: 39.3 us -> 9.98 us
  between operations: 14.9 us -> 0.66 us
  other arithmetic: 10.4 us -> 3.65 us
  starting transfers between devices: 6.15 us -> 0 us
    unnamed x4 -> x0, waiting for transfers between devices: 154 us -> none
    pallas_call x0 -> x1, Pallas kernels: none -> 85.7 us  [per_device(): pl.pallas_call(kernel, out_shape=(jax.ShapeDtypeStruct(line, F32), jax.Sh...]
    dot_general x7 -> x0, matrix products: 50.3 us -> none  [the longest x1 15.8 us: per_device(): jnp.einsum('hrk,hrj->khj', act_one, delta_two, preferred_element_type=jnp...]
    unnamed x31 -> x5, local copies, waits for them, and re-layouts: 25.7 us -> 4.43 us
    all_to_all x1 -> x0, starting transfers between devices: 6.07 us -> none  [sent_to_all(): return lax.all_to_all(copies, axis, split_axis=0, concat_axis=0, tiled=True)]
    convert_element_type x2 -> x0, local copies, waits for them, and re-layouts: 4.78 us -> none  [the longest x1 3.94 us: per_device(): grad_in.astype(jnp.bfloat16)]
    reduce_sum x1 -> x0, other arithmetic: 4.04 us -> none  [per_device(): grad_two = jnp.sum(delta_two.astype(jnp.float32), axis=1)]
    all_to_all x1 -> x0, waiting for transfers between devices: 3.4 us -> none  [sent_to_all(): return lax.all_to_all(copies, axis, split_axis=0, concat_axis=0, tiled=True)]
  transfers between devices with their start and end apart: 3 -> 0, of which waited for: 3 -> 0; matrix products, arithmetic and copies ran while one was open for 16% -> 0% of each run, Pallas kernels for 0% -> 0%
where the time goes in v1:
time: 100 us
  Pallas kernels  85.7 us (86%)
  local copies, waits for them, and re-layouts  9.98 us (10%)
  other arithmetic  3.65 us (4%)
    pallas_call x1, Pallas kernels, per_device(): pl.pallas_call(kernel, out_shape=(jax.ShapeDtypeStruct(line, F32), jax.Sh...  85.7 us
    unnamed x5, local copies, waits for them, and re-layouts  4.43 us

profile of v1, /device:TPU:1, one launch (start us, length us, event | category | flops | bytes accessed | tf_op | source)
XLA Modules:
  0.0 100.0 jit_solution(11475621935244452947)
XLA Ops:
  0.6 1.2 %reshape.25.reward = f32[1,384]{1,0:T(1,128)} reshape(f32[384]{0:T(512)} %param.10) | data formatting | bytes 3072 | tf_op jit(solution)/shard_map/reshape | solution.py:350
  1.9 1.2 %reshape.26.done = s32[1,384]{1,0:T(1,128)} reshape(s32[384]{0:T(512)} %param.11) | data formatting | bytes 3072 | tf_op jit(solution)/shard_map/reshape | solution.py:350
  3.1 1.2 %reshape.27.vnext = f32[1,384]{1,0:T(1,128)} reshape(f32[384]{0:T(512)} %param.12) | data formatting | bytes 3072 | tf_op jit(solution)/shard_map/reshape | solution.py:350
  4.4 1.2 %reshape.28.vnow = f32[1,384]{1,0:T(1,128)} reshape(f32[384]{0:T(512)} %param.13) | data formatting | bytes 3072 | tf_op jit(solution)/shard_map/reshape | solution.py:351
  5.6 85.7 %shard_map.128 = (f32[1,384]{1,0:T(1,128)}, bf16[2,128,2048]{2,1,0:T(8,128)(2,1)}, bf16[2,16,2304]{2,1,0:T(8,128)(2,1)}) custom-call(bf16[384,256]{1,0:T(8,128)(2,1)} %feat_hbm.1, f32[1,384]{1,0:T(1,128)} %reshape.25.reward, s32[1,384]{1,0:T(1,128)} %reshape.26.done, f32[1,384]{1,0:T(1,128)} %reshape.27.vnext, f32[1,384]{1,0:T(1,128)} %reshape.28.vnow, ...), custom_call_target="tpu_custom_call" | custom-call | tf_op jit(solution)/shard_map/pallas_call | solution.py:303
  91.3 0.7 slice_convert_fusion
  92.0 0.6 copy.16
  92.6 0.6 slice.17
  93.1 0.9 convert_bitcast_fusion.1
  94.1 0.9 copy.14
  95.0 1.5 %convert_bitcast_fusion = f32[128,2,2048]{2,0,1:T(8,128)S(1)} fusion(bf16[2,128,2048]{2,1,0:T(8,128)(2,1)} %get-tuple-element.10), kind=kLoop, calls=%fused_computation | loop fusion | flops 524288 | bytes 3145728 | tf_op jit(solution)/shard_map/convert_element_type | solution.py:353
  96.4 0.0 copy-start
  96.4 2.9 %copy.15 = f32[128,2,2048]{2,1,0:T(2,128)} copy(f32[128,2,2048]{2,0,1:T(8,128)S(1)} %convert_bitcast_fusion) | data formatting | bytes 4194304
  99.4 0.0 copy-done
  99.4 0.6 reduce
  (1 shorter events, 0.0 us)
Async XLA Ops:
  96.4 3.0 %copy-start = (f32[1,384]{1,0:T(1,128)S(1)}, f32[1,384]{1,0:T(1,128)}, u32[]{:S(2)}) copy-start(f32[1,384]{1,0:T(1,128)} %get-tuple-element.8) | copy-start | bytes 4612

commit v2 on v1

--- a/solution.py
+++ b/solution.py
@@ -14,6 +14,10 @@
 R2 = 2 * ROWS
 C = 256
 NC = H // C
+C1 = 512
+C2 = 512
+C3 = 512
+C5 = 512
 GW = H + 256
 HALF = H // 2
 GH = GW // 2
@@ -80,7 +84,7 @@
         pl.semaphore_signal(barrier, inc=1, device_id=p, device_id_type=MESH)
 
     target = reward[...] + 0.99 * (1.0 - done[...].astype(F32)) * vnext[...]
-    tgt[...] = jnp.broadcast_to(target, (8, ROWS))
+    tgt[...] = jnp.broadcast_to(target.reshape(1, ROWS), (8, ROWS))
     pl.semaphore_wait(barrier, len(partners))
 
     copies = []
@@ -120,9 +124,9 @@
         if p == 1:
             got_feat.wait_recv()
 
-        @pl.loop(0, NC)
+        @pl.loop(0, H // C1)
         def _(n):
-            cols = chunk(n)
+            cols = chunk(n, C1)
             val = tn(feat[rows, :], win[:, cols]) + stats[0:1, cols]
             act, slope = silu_both(val)
             act1[rows, cols] = act.astype(BF)
@@ -133,14 +137,14 @@
             for copy in loads[2:]:
                 copy.wait()
 
-        @pl.loop(0, NC)
+        @pl.loop(0, H // C2)
         def _(n):
-            cols = chunk(n)
+            cols = chunk(n, C2)
             val = tn(act1[rows, :], wmid[:, cols]) + stats[1:2, cols]
             act, slope = silu_both(val)
             wrow = stats[2:3, cols]
             prod = act * wrow
-            accq[rows, :] += prod[:, :128] + prod[:, 128:]
+            accq[rows, :] += sum(prod[:, i * 128 : (i + 1) * 128] for i in range(C2 // 128))
             act2[rows, cols] = act.astype(BF)
             sl2[rows, cols] = (slope * wrow).astype(BF)
 
@@ -153,10 +157,10 @@
     eb[...] = jnp.transpose(jnp.broadcast_to(err[0:1], (128, R2)))
     stats[...] = jnp.zeros_like(stats)
 
-    @pl.loop(0, NC)
+    @pl.loop(0, H // C3)
     def _(n):
-        cols = chunk(n)
-        e = jnp.concatenate([eb[...], eb[...]], axis=1)
+        cols = chunk(n, C3)
+        e = jnp.concatenate([eb[...]] * (C3 // 128), axis=1)
         d = e * sl2[:, cols].astype(F32)
         del2[:, cols] = d.astype(BF)
         stats[1:2, cols] = jnp.sum(d, axis=0, keepdims=True)
@@ -169,12 +173,10 @@
             lhs[pl.ds(rv * 128, 128), :] = jnp.transpose(act1[:, chunk(dp_of(ru, rv), 128)])
 
     def products(ru, half):
-        @pl.loop(half * NC // 2, (half + 1) * NC // 2)
-        def _(n):
-            cols = chunk(n)
-            res = tn(lhs[...], del2[:, cols]).astype(BF)
-            for rv in range(4):
-                part[ru, rv, :, cols] = res[rv * 128 : (rv + 1) * 128]
+        cols = pl.ds(half * HALF, HALF)
+        res = tn(lhs[...], del2[:, cols]).astype(BF)
+        for rv in range(4):
+            part[ru, rv, :, cols] = res[rv * 128 : (rv + 1) * 128]
 
     left, right = pl.ds(0, HALF), pl.ds(HALF, HALF)
     one_a, one_b, two_a, two_b = [None] * 4, [None] * 4, [None] * 4, [None] * 4
@@ -214,9 +216,9 @@
 
     featT[...] = jnp.transpose(feat[...])
 
-    @pl.loop(0, NC)
+    @pl.loop(0, H // C5)
     def _(n):
-        cols = chunk(n)
+        cols = chunk(n, C5)
         back = nt(del2[...], wmid[cols, :])
         d = back * sl1[:, cols].astype(F32)
         stats[0:1, cols] = jnp.sum(d, axis=0, keepdims=True)
@@ -250,50 +252,72 @@
     gp[4:8, :, gr] = (gp[4:8, :, gr].astype(F32) + g1b[...].astype(F32)).astype(BF)
     g_two_a.append(send(gp.at[pl.ds(4, 4), :, gr], g2a.at[:, :, gr], u1))
 
-    def ring_sum(rv):
-        for copy in (*two_a[rv], *two_b[rv]):
-            copy.wait_recv()
-        part[0, rv] = (part[0, rv].astype(F32) + r2a[rv].astype(F32) + r2b[rv].astype(F32)).astype(BF)
-
-    ring_sum(2)
-    three_3 = send(part.at[0, 2], r3.at[1], v1)
-    ring_sum(1)
-    three_0 = send(part.at[0, 1], r3.at[0], v1)
-    ring_sum(3)
-    three_3.wait_recv()
-    part[0, 3] = (part[0, 3].astype(F32) + r3[1].astype(F32)).astype(BF)
-    four = send(part.at[0, 3], mid_out.at[head], v3)
+    sides = (left, right)
+
+    def ring_sum(rv, half):
+        two_a[rv][half].wait_recv()
+        two_b[rv][1 - half].wait_recv()
+        at = sides[half]
+        return part[0, rv, :, at].astype(F32) + r2a[rv, :, at].astype(F32) + r2b[rv, :, at].astype(F32)
+
+    three = {}
+    for rv, slot in ((2, 1), (1, 0)):
+        for half, at in enumerate(sides):
+            part[0, rv, :, at] = ring_sum(rv, half).astype(BF)
+            three[slot, half] = send(part.at[0, rv, :, at], r3.at[slot, :, at], v1)
+    four = []
+    for half, at in enumerate(sides):
+        total = ring_sum(3, half)
+        three[1, half].wait_recv()
+        part[0, 3, :, at] = (total + r3[1, :, at].astype(F32)).astype(BF)
+        four.append(send(part.at[0, 3, :, at], mid_out.at[head, :, at], v3))
 
     for copy in (*g_two_a, *g_two_b):
         copy.wait_recv()
     gp[0:4] = (gp[0:4].astype(F32) + g2a[...].astype(F32) + g2b[...].astype(F32)).astype(BF)
     g_three = send(gp.at[pl.ds(1, 2)], g3, v1)
 
-    ring_sum(0)
-    three_0.wait_recv()
-    part[0, 0] = (part[0, 0].astype(F32) + r3[0].astype(F32)).astype(BF)
-    own_mid = pltpu.make_async_copy(part.at[0, 0], mid_out.at[head], osem.at[0])
-    own_mid.start()
+    own_mid = []
+    for half, at in enumerate(sides):
+        total = ring_sum(0, half)
+        three[0, half].wait_recv()
+        part[0, 0, :, at] = (total + r3[0, :, at].astype(F32)).astype(BF)
+        copy = pltpu.make_async_copy(part.at[0, 0, :, at], mid_out.at[head, :, at], osem.at[half])
+        copy.start()
+        own_mid.append(copy)
 
     g_three.wait_recv()
     gp[3] = (gp[3].astype(F32) + g3[1].astype(F32)).astype(BF)
     g_four = send(gp.at[3], gin_out.at[head], v3)
     gp[0] = (gp[0].astype(F32) + g3[0].astype(F32)).astype(BF)
-    own_gin = pltpu.make_async_copy(gp.at[0], gin_out.at[head], osem.at[1])
+    own_gin = pltpu.make_async_copy(gp.at[0], gin_out.at[head], osem.at[2])
     own_gin.start()
 
     for copy in got_x:
         copy.wait_recv()
     q_min = jnp.minimum(jnp.minimum(mm[...], mx[0]), jnp.minimum(mx[1], mx[2]))
-    gap = q_min[0:1] - vnow[...]
+    gap = q_min[0:1] - vnow[...].reshape(1, ROWS)
     vg_out[...] = -2.0 * jnp.where(gap < 0.0, 0.3, 0.7) * gap
 
-    own_mid.wait()
+    for copy in own_mid:
+        copy.wait()
     own_gin.wait()
-    four.wait_recv()
+    for copy in four:
+        copy.wait_recv()
     g_four.wait_recv()
     for copy in copies:
         copy.wait_send()
+
+
+def finish(vg, mid, gin, vg_out, din, dmid, dbias, dout):
+    vg_out[...] = vg[...].reshape(ROWS)
+    for h in range(2):
+        dmid[:, h, :] = mid[h].astype(F32)
+        din[:, h, :] = gin[h, :, :H].astype(F32)
+        rest = gin[h, :, H : H + 128].astype(F32)
+        dbias[0, h : h + 1, :] = rest[0:1]
+        dbias[1, h : h + 1, :] = rest[1:2]
+        dout[h : h + 1, :] = rest[2:3]
 
 
 def per_device(features, reward, done, value_next, value_now, w_in, w_mid, biases, w_out):
@@ -339,22 +363,28 @@
             pltpu.VMEM((3, 8, ROWS), F32),
             pltpu.SemaphoreType.DMA((2,)),
             pltpu.SemaphoreType.DMA((NC,)),
-            pltpu.SemaphoreType.DMA((2,)),
-            pltpu.SemaphoreType.DMA((48,)),
-            pltpu.SemaphoreType.DMA((48,)),
+            pltpu.SemaphoreType.DMA((3,)),
+            pltpu.SemaphoreType.DMA((56,)),
+            pltpu.SemaphoreType.DMA((56,)),
         ],
         compiler_params=pltpu.CompilerParams(
             collective_id=0, has_side_effects=True, vmem_limit_bytes=67_000_000
         ),
     )(
-        features, reward.reshape(line), done.reshape(line), value_next.reshape(line),
-        value_now.reshape(line), w_in, w_mid, biases, w_out,
+        features, reward, done, value_next, value_now, w_in, w_mid, biases, w_out,
     )
-    d_mid = jnp.transpose(mid, (1, 0, 2)).astype(F32)
-    d_in = jnp.transpose(gin[:, :, :H], (1, 0, 2)).astype(F32)
-    rest = gin[:, :3, H : H + 128].astype(F32)
-    d_bias = jnp.transpose(rest[:, :2], (1, 0, 2))
-    return vg.reshape(ROWS), d_in, d_mid, d_bias, rest[:, 2]
+    return pl.pallas_call(
+        finish,
+        out_shape=(
+            jax.ShapeDtypeStruct((ROWS,), F32),
+            jax.ShapeDtypeStruct((16, 2, H), F32),
+            jax.ShapeDtypeStruct((128, 2, H), F32),
+            jax.ShapeDtypeStruct((2, 2, 128), F32),
+            jax.ShapeDtypeStruct((2, 128), F32),
+        ),
+        in_specs=[vm, vm, vm],
+        out_specs=(vm,) * 5,
+    )(vg, mid, gin)
 
 
 def solution(mesh):

time: 100 us -> 87.2 us (0.87); the launches traced: 100 us -> 86.1 us
  local copies, waits for them, and re-layouts: 9.98 us -> 0 us
  other arithmetic: 3.65 us -> 0 us
    reshape x4 -> x0, local copies, waits for them, and re-layouts: 4.98 us -> none  [the longest x1 1.25 us: per_device(): reward.reshape(line)]
    unnamed x5 -> x0, local copies, waits for them, and re-layouts: 4.43 us -> none
    pallas_call x1, Pallas kernels: 85.7 us -> 82.4 us  [per_device(): pl.pallas_call(kernel, out_shape=(jax.ShapeDtypeStruct(line, F32), jax.Sh...]
    convert_element_type x3 -> x0, other arithmetic: 3.05 us -> none  [the longest x1 1.45 us: per_device(): d_mid = jnp.transpose(mid, (1, 0, 2)).astype(F32)]
    pallas_call x0 -> x1, Pallas kernels: none -> 3.01 us  [per_device(): pl.pallas_call(finish, out_shape=(jax.ShapeDtypeStruct((ROWS,), F32), jax...]
where the time goes in v2:
time: 87.2 us; the launch traced here: 86.1 us
  Pallas kernels  85.4 us (98%)
    pallas_call x1, Pallas kernels, per_device(): pl.pallas_call(kernel, out_shape=(jax.ShapeDtypeStruct(line, F32), jax.Sh...  82.4 us
    pallas_call x1, Pallas kernels, per_device(): pl.pallas_call(finish, out_shape=(jax.ShapeDtypeStruct((ROWS,), F32), jax...  3.01 us

profile of v2, /device:TPU:1, one launch (start us, length us, event | category | flops | bytes accessed | tf_op | source)
XLA Modules:
  0.0 86.1 jit_solution(14693822044463557644)
XLA Ops:
  0.6 82.4 %shard_map.128 = (f32[1,384]{1,0:T(1,128)}, bf16[2,128,2048]{2,1,0:T(8,128)(2,1)}, bf16[2,16,2304]{2,1,0:T(8,128)(2,1)}) custom-call(bf16[384,256]{1,0:T(8,128)(2,1)} %feat_hbm.1, f32[384]{0:T(512)} %reward.1, s32[384]{0:T(512)} %done.1, f32[384]{0:T(512)} %vnext.1, f32[384]{0:T(512)} %vnow.1, bf16[2,256,2048]{2,1,0:T(8,128)(2,1)} %win_hbm.1, ...), custom_call_target="tpu_custom_call" | custom-call | tf_op jit(solution)/shard_map/pallas_call | solution.py:327
  83.0 3.0 %shard_map.129 = (f32[384]{0:T(512)}, f32[16,2,2048]{2,1,0:T(2,128)}, f32[128,2,2048]{2,1,0:T(2,128)}, f32[2,2,128]{2,1,0:T(2,128)}, f32[2,128]{1,0:T(2,128)}) custom-call(f32[1,384]{1,0:T(1,128)} %get-tuple-element.8.vg, bf16[2,128,2048]{2,1,0:T(8,128)(2,1)} %get-tuple-element.9.mid, bf16[2,16,2304]{2,1,0:T(8,128)(2,1)} %get-tuple-element.10.gin), custom_call_target="tpu_custom_call" | custom-call | tf_op jit(solution)/shard_map/pallas_call | solution.py:376

commit v3 on v2

--- a/solution.py
+++ b/solution.py
@@ -18,9 +18,11 @@
 C2 = 512
 C3 = 512
 C5 = 512
-GW = H + 256
-HALF = H // 2
-GH = GW // 2
+GW = H + 128
+LEFT = 768
+RIGHT = H - LEFT
+GL = 896
+GR = GW - GL
 
 
 def tn(a, b, **kw):
@@ -36,11 +38,11 @@
 
 
 def kernel(
-    feat_hbm, reward, done, vnext, vnow, win_hbm, wmid_hbm, biases, wout,
+    feat_hbm, reward_hbm, done_hbm, vnext_hbm, vnow_hbm, win_hbm, wmid_hbm, biases_hbm, wout_hbm,
     vg_out, mid_out, gin_out,
-    feat, win, wmid, act1, sl1, act2, sl2, del2, accq, eb, stats, part, lhs, featT,
+    feat, win, wmid, act1, sl1, act2, sl2, del2, accq, eb, stats, part, actT, featT,
     r1a, r1b, r2a, r2b, r3, gp, g1a, g1b, g2a, g2b, g3,
-    tgt, tgtm, qm, qr, mo, ms, mm, mx,
+    reward, done, vnext, vnow, biases, wout, tgt, tgtm, qm, qr, mo, ms, mm, mx,
     lsem, wsem, osem, ssem, rsem,
 ):
     ens = lax.axis_index("ens")
@@ -65,6 +67,11 @@
     sib = (ens ^ 1, dp)
     xs = [((xpos ^ k) * 2 + core, dp) for k in (1, 2, 3)]
 
+    barrier = pltpu.get_barrier_semaphore()
+    partners = [u1, u3, v1, v3, sib, *xs]
+    for p in partners:
+        pl.semaphore_signal(barrier, inc=1, device_id=p, device_id_type=MESH)
+
     loads = [
         pltpu.make_async_copy(feat_hbm, feat.at[pl.ds(0, ROWS)], lsem.at[0]),
         pltpu.make_async_copy(win_hbm.at[head], win, lsem.at[1]),
@@ -75,16 +82,59 @@
                 wmid_hbm.at[head, :, pl.ds(n * C, C)], wmid.at[:, pl.ds(n * C, C)], wsem.at[n]
             )
         )
-    for copy in loads:
+    for copy in loads[:2]:
         copy.start()
 
-    barrier = pltpu.get_barrier_semaphore()
-    partners = [u1, u3, v1, v3, sib, *xs]
-    for p in partners:
-        pl.semaphore_signal(barrier, inc=1, device_id=p, device_id_type=MESH)
-
+    small = [
+        pltpu.make_async_copy(src, dst, lsem.at[2 + i])
+        for i, (src, dst) in enumerate(
+            (
+                (biases_hbm, biases), (wout_hbm, wout), (reward_hbm, reward), (done_hbm, done),
+                (vnext_hbm, vnext), (vnow_hbm, vnow),
+            )
+        )
+    ]
+    for copy in small:
+        copy.start()
+
+    for copy in loads[2:]:
+        copy.start()
+
+    for copy in small:
+        copy.wait()
     target = reward[...] + 0.99 * (1.0 - done[...].astype(F32)) * vnext[...]
     tgt[...] = jnp.broadcast_to(target.reshape(1, ROWS), (8, ROWS))
+    loads[0].wait()
+    loads[1].wait()
+
+    wo = wout[...].astype(F32)
+    wo = jnp.where(head == 0, wo[0:1], wo[1:2])
+    b_all = biases[...]
+    b_one = jnp.where(head == 0, b_all[0, 0:1], b_all[0, 1:2])
+    b_two = jnp.where(head == 0, b_all[1, 0:1], b_all[1, 1:2])
+    stats[...] = jnp.zeros_like(stats)
+    stats[0:1, :] = b_one
+    stats[1:2, :] = b_two
+    stats[2:3, :] = wo
+
+    def silu_both(val):
+        s = 0.5 * jnp.tanh(0.5 * val) + 0.5
+        act = val * s
+        return act, s + act * (1.0 - s)
+
+    accq[...] = jnp.zeros_like(accq)
+
+    def layer_one(p):
+        rows = pl.ds(p * ROWS, ROWS)
+
+        @pl.loop(0, H // C1)
+        def _(n):
+            cols = chunk(n, C1)
+            val = tn(feat[rows, :], win[:, cols]) + stats[0:1, cols]
+            act, slope = silu_both(val)
+            act1[rows, cols] = act.astype(BF)
+            sl1[rows, cols] = slope.astype(BF)
+
     pl.semaphore_wait(barrier, len(partners))
 
     copies = []
@@ -99,47 +149,18 @@
         copy.start()
         return copy
 
-    loads[0].wait()
     got_feat = send(feat.at[pl.ds(0, ROWS)], feat.at[pl.ds(ROWS, ROWS)], v3)
     got_tgt = send(tgt, tgtm, v3)
-    loads[1].wait()
-
-    wo = wout[...].astype(F32)
-    wo = jnp.where(head == 0, wo[0:1], wo[1:2])
-    b_all = biases[...]
-    b_one = jnp.where(head == 0, b_all[0, 0:1], b_all[0, 1:2])
-    b_two = jnp.where(head == 0, b_all[1, 0:1], b_all[1, 1:2])
-    stats[...] = jnp.zeros_like(stats)
-    stats[0:1, :] = b_one
-    stats[1:2, :] = b_two
-    stats[2:3, :] = wo
-
-    def silu_both(val):
-        s = 0.5 * jnp.tanh(0.5 * val) + 0.5
-        act = val * s
-        return act, s + act * (1.0 - s)
-
-    for p in range(2):
+    def layer_two(p):
         rows = pl.ds(p * ROWS, ROWS)
-        if p == 1:
-            got_feat.wait_recv()
-
-        @pl.loop(0, H // C1)
-        def _(n):
-            cols = chunk(n, C1)
-            val = tn(feat[rows, :], win[:, cols]) + stats[0:1, cols]
-            act, slope = silu_both(val)
-            act1[rows, cols] = act.astype(BF)
-            sl1[rows, cols] = slope.astype(BF)
-
-        accq[rows, :] = jnp.zeros((ROWS, 128), F32)
-        if p == 0:
-            for copy in loads[2:]:
-                copy.wait()
 
         @pl.loop(0, H // C2)
         def _(n):
             cols = chunk(n, C2)
+            if p == 1:
+                for i in range(C2 // 128):
+                    d = n * (C2 // 128) + i
+                    actT[d] = jnp.transpose(act1[:, chunk(d, 128)])
             val = tn(act1[rows, :], wmid[:, cols]) + stats[1:2, cols]
             act, slope = silu_both(val)
             wrow = stats[2:3, cols]
@@ -147,6 +168,14 @@
             accq[rows, :] += sum(prod[:, i * 128 : (i + 1) * 128] for i in range(C2 // 128))
             act2[rows, cols] = act.astype(BF)
             sl2[rows, cols] = (slope * wrow).astype(BF)
+
+    layer_one(0)
+    for copy in loads[2:]:
+        copy.wait()
+    layer_two(0)
+    got_feat.wait_recv()
+    layer_one(1)
+    layer_two(1)
 
     q = nt(jnp.ones((8, 128), F32), accq[...], precision=lax.Precision.HIGHEST)
     got_tgt.wait_recv()
@@ -168,51 +197,45 @@
 
     order = (2, 1, 3, 0)
 
-    def group(ru):
+    def products(ru, side):
+        rows = jnp.concatenate([actT[dp_of(ru, rv)] for rv in range(4)], axis=0)
+        res = tn(rows, del2[:, side]).astype(BF)
         for rv in range(4):
-            lhs[pl.ds(rv * 128, 128), :] = jnp.transpose(act1[:, chunk(dp_of(ru, rv), 128)])
-
-    def products(ru, half):
-        cols = pl.ds(half * HALF, HALF)
-        res = tn(lhs[...], del2[:, cols]).astype(BF)
-        for rv in range(4):
-            part[ru, rv, :, cols] = res[rv * 128 : (rv + 1) * 128]
-
-    left, right = pl.ds(0, HALF), pl.ds(HALF, HALF)
+            part[ru, rv, :, side] = res[rv * 128 : (rv + 1) * 128]
+
+    left, right = pl.ds(0, LEFT), pl.ds(LEFT, RIGHT)
     one_a, one_b, two_a, two_b = [None] * 4, [None] * 4, [None] * 4, [None] * 4
-    group(2)
-    products(2, 0)
-    for rv in order:
-        one_a[rv] = send(part.at[2, rv, :, left], r1a.at[rv], u1)
-    products(2, 1)
-    for rv in order:
-        one_b[rv] = send(part.at[2, rv, :, right], r1b.at[rv], u3)
-    group(1)
-    products(1, 0)
-    for rv in order:
-        two_a[rv] = [send(part.at[1, rv, :, left], r2a.at[rv, :, left], u1)]
-    products(1, 1)
-    group(3)
-    products(3, 1)
-    for rv in order:
-        two_b[rv] = [send(part.at[3, rv, :, right], r2b.at[rv, :, right], u3)]
-    products(3, 0)
-    group(0)
-    products(0, 0)
-    products(0, 1)
-
-    got_q.wait_recv()
-    mo[...] = jnp.minimum(mo[...], qr[...])
-    got_sib = send(mo, ms, sib)
-
-    def merge():
-        for rv in order:
+    first, last = (2, 1), (3, 0)
+
+    def step_one(side, rvs):
+        for rv in rvs:
+            if side == 0:
+                one_a[rv] = send(part.at[2, rv, :, left], r1a.at[rv], u1)
+            else:
+                one_b[rv] = send(part.at[2, rv, :, right], r1b.at[rv], u3)
+
+    def raw(side, rvs):
+        for rv in rvs:
+            if side == 0:
+                two_a[rv] = [send(part.at[1, rv, :, left], r2a.at[rv, :, left], u1)]
+            else:
+                two_b[rv] = [send(part.at[3, rv, :, right], r2b.at[rv, :, right], u3)]
+
+    def merge(rvs):
+        for rv in rvs:
             one_a[rv].wait_recv()
             part[3, rv, :, left] = (part[3, rv, :, left].astype(F32) + r1a[rv].astype(F32)).astype(BF)
             two_b[rv].append(send(part.at[3, rv, :, left], r2b.at[rv, :, left], u3))
             one_b[rv].wait_recv()
             part[1, rv, :, right] = (part[1, rv, :, right].astype(F32) + r1b[rv].astype(F32)).astype(BF)
             two_a[rv].append(send(part.at[1, rv, :, right], r2a.at[rv, :, right], u1))
+
+    products(2, right)
+    step_one(1, order)
+    products(2, left)
+    step_one(0, order)
+    products(1, left)
+    raw(0, first)
 
     featT[...] = jnp.transpose(feat[...])
 
@@ -231,26 +254,36 @@
         slot = jnp.where(core == 0, (i // 4 ^ y) * 4 + (i % 4 ^ z), (i % 4 ^ z) * 4 + (i // 4 ^ y))
         tile = jnp.concatenate([stats[:, i * 128 : (i + 1) * 128], jnp.zeros((8, 128), F32)], axis=0)
         gp[slot, :, pl.ds(H, 128)] = tile.astype(BF)
-        gp[slot, :, pl.ds(H + 128, 128)] = jnp.zeros((16, 128), BF)
-
-    got_sib.wait_recv()
-    mm[...] = jnp.minimum(mo[...], ms[...])
-    got_x = [send(mm, mx.at[k], xs[k]) for k in range(3)]
-
-    gl, gr = pl.ds(0, GH), pl.ds(GH, GH)
+
+    gl, gr = pl.ds(0, GL), pl.ds(GL, GR)
     g_one_a = send(gp.at[pl.ds(8, 4), :, gl], g1a, u1)
     g_one_b = send(gp.at[pl.ds(8, 4), :, gr], g1b, u3)
     g_two_a = [send(gp.at[pl.ds(4, 4), :, gl], g2a.at[:, :, gl], u1)]
     g_two_b = [send(gp.at[pl.ds(12, 4), :, gr], g2b.at[:, :, gr], u3)]
 
-    merge()
-
+    got_q.wait_recv()
+    mo[...] = jnp.minimum(mo[...], qr[...])
+    got_sib = send(mo, ms, sib)
+
+    products(3, right)
+    raw(1, first)
+    products(1, right)
+    products(3, left)
     g_one_a.wait_recv()
     gp[12:16, :, gl] = (gp[12:16, :, gl].astype(F32) + g1a[...].astype(F32)).astype(BF)
     g_two_b.append(send(gp.at[pl.ds(12, 4), :, gl], g2b.at[:, :, gl], u3))
     g_one_b.wait_recv()
     gp[4:8, :, gr] = (gp[4:8, :, gr].astype(F32) + g1b[...].astype(F32)).astype(BF)
     g_two_a.append(send(gp.at[pl.ds(4, 4), :, gr], g2a.at[:, :, gr], u1))
+    merge(first)
+    raw(0, last)
+    raw(1, last)
+    merge(last)
+    got_sib.wait_recv()
+    mm[...] = jnp.minimum(mo[...], ms[...])
+    got_x = [send(mm, mx.at[k], xs[k]) for k in range(3)]
+    products(0, left)
+    products(0, right)
 
     sides = (left, right)
 
@@ -265,6 +298,11 @@
         for half, at in enumerate(sides):
             part[0, rv, :, at] = ring_sum(rv, half).astype(BF)
             three[slot, half] = send(part.at[0, rv, :, at], r3.at[slot, :, at], v1)
+    for copy in (*g_two_a, *g_two_b):
+        copy.wait_recv()
+    gp[0:4] = (gp[0:4].astype(F32) + g2a[...].astype(F32) + g2b[...].astype(F32)).astype(BF)
+    g_three = send(gp.at[pl.ds(1, 2)], g3, v1)
+
     four = []
     for half, at in enumerate(sides):
         total = ring_sum(3, half)
@@ -272,10 +310,12 @@
         part[0, 3, :, at] = (total + r3[1, :, at].astype(F32)).astype(BF)
         four.append(send(part.at[0, 3, :, at], mid_out.at[head, :, at], v3))
 
-    for copy in (*g_two_a, *g_two_b):
-        copy.wait_recv()
-    gp[0:4] = (gp[0:4].astype(F32) + g2a[...].astype(F32) + g2b[...].astype(F32)).astype(BF)
-    g_three = send(gp.at[pl.ds(1, 2)], g3, v1)
+    g_three.wait_recv()
+    gp[3] = (gp[3].astype(F32) + g3[1].astype(F32)).astype(BF)
+    g_four = send(gp.at[3], gin_out.at[head], v3)
+    gp[0] = (gp[0].astype(F32) + g3[0].astype(F32)).astype(BF)
+    own_gin = pltpu.make_async_copy(gp.at[0], gin_out.at[head], osem.at[2])
+    own_gin.start()
 
     own_mid = []
     for half, at in enumerate(sides):
@@ -286,13 +326,6 @@
         copy.start()
         own_mid.append(copy)
 
-    g_three.wait_recv()
-    gp[3] = (gp[3].astype(F32) + g3[1].astype(F32)).astype(BF)
-    g_four = send(gp.at[3], gin_out.at[head], v3)
-    gp[0] = (gp[0].astype(F32) + g3[0].astype(F32)).astype(BF)
-    own_gin = pltpu.make_async_copy(gp.at[0], gin_out.at[head], osem.at[2])
-    own_gin.start()
-
     for copy in got_x:
         copy.wait_recv()
     q_min = jnp.minimum(jnp.minimum(mm[...], mx[0]), jnp.minimum(mx[1], mx[2]))
@@ -310,14 +343,18 @@
 
 
 def finish(vg, mid, gin, vg_out, din, dmid, dbias, dout):
-    vg_out[...] = vg[...].reshape(ROWS)
     for h in range(2):
         dmid[:, h, :] = mid[h].astype(F32)
-        din[:, h, :] = gin[h, :, :H].astype(F32)
-        rest = gin[h, :, H : H + 128].astype(F32)
-        dbias[0, h : h + 1, :] = rest[0:1]
-        dbias[1, h : h + 1, :] = rest[1:2]
-        dout[h : h + 1, :] = rest[2:3]
+
+    @pl.when(pl.program_id(0) == 0)
+    def _():
+        vg_out[...] = vg[...].reshape(ROWS)
+        for h in range(2):
+            din[:, h, :] = gin[h, :, :H].astype(F32)
+            rest = gin[h, :, H:].astype(F32)
+            dbias[0, h : h + 1, :] = rest[0:1]
+            dbias[1, h : h + 1, :] = rest[1:2]
+            dout[h : h + 1, :] = rest[2:3]
 
 
 def per_device(features, reward, done, value_next, value_now, w_in, w_mid, biases, w_out):
@@ -331,7 +368,7 @@
             jax.ShapeDtypeStruct((2, 128, H), BF),
             jax.ShapeDtypeStruct((2, 16, GW), BF),
         ),
-        in_specs=[hbm, vm, vm, vm, vm, hbm, hbm, vm, vm],
+        in_specs=[hbm] * 9,
         out_specs=(vm, hbm, hbm),
         scratch_shapes=[
             pltpu.VMEM((R2, IN), BF),
@@ -346,22 +383,28 @@
             pltpu.VMEM((R2, 128), F32),
             pltpu.VMEM((8, H), F32),
             pltpu.VMEM((4, 4, 128, H), BF),
-            pltpu.VMEM((512, R2), BF),
+            pltpu.VMEM((16, 128, R2), BF),
             pltpu.VMEM((IN, R2), BF),
-            pltpu.VMEM((4, 128, HALF), BF),
-            pltpu.VMEM((4, 128, HALF), BF),
+            pltpu.VMEM((4, 128, LEFT), BF),
+            pltpu.VMEM((4, 128, RIGHT), BF),
             pltpu.VMEM((4, 128, H), BF),
             pltpu.VMEM((4, 128, H), BF),
             pltpu.VMEM((2, 128, H), BF),
             pltpu.VMEM((16, 16, GW), BF),
-            pltpu.VMEM((4, 16, GH), BF),
-            pltpu.VMEM((4, 16, GH), BF),
+            pltpu.VMEM((4, 16, GL), BF),
+            pltpu.VMEM((4, 16, GR), BF),
             pltpu.VMEM((4, 16, GW), BF),
             pltpu.VMEM((4, 16, GW), BF),
             pltpu.VMEM((2, 16, GW), BF),
+            pltpu.VMEM((ROWS,), F32),
+            pltpu.VMEM((ROWS,), jnp.int32),
+            pltpu.VMEM((ROWS,), F32),
+            pltpu.VMEM((ROWS,), F32),
+            pltpu.VMEM((2, 2, H), F32),
+            pltpu.VMEM((2, H), BF),
             *[pltpu.VMEM((8, ROWS), F32)] * 7,
             pltpu.VMEM((3, 8, ROWS), F32),
-            pltpu.SemaphoreType.DMA((2,)),
+            pltpu.SemaphoreType.DMA((8,)),
             pltpu.SemaphoreType.DMA((NC,)),
             pltpu.SemaphoreType.DMA((3,)),
             pltpu.SemaphoreType.DMA((56,)),
@@ -382,8 +425,9 @@
             jax.ShapeDtypeStruct((2, 2, 128), F32),
             jax.ShapeDtypeStruct((2, 128), F32),
         ),
-        in_specs=[vm, vm, vm],
-        out_specs=(vm,) * 5,
+        grid=(4,),
+        in_specs=[vm, pl.BlockSpec((2, 32, H), lambda i: (0, i, 0)), vm],
+        out_specs=(vm, vm, pl.BlockSpec((32, 2, H), lambda i: (i, 0, 0)), vm, vm),
     )(vg, mid, gin)
 
 

time: 87.2 us -> 86.8 us (level); the launches traced: 86.1 us -> 86.7 us
    pallas_call x1, Pallas kernels: 3.01 us -> 3.92 us  [per_device(): pl.pallas_call(finish, out_shape=(jax.ShapeDtypeStruct((ROWS,), F32), jax...]
where the time goes in v3:
time: 86.8 us; the launch traced here: 86.7 us
  Pallas kernels  86 us (99%)
    pallas_call x1, Pallas kernels, per_device(): pl.pallas_call(kernel, out_shape=(jax.ShapeDtypeStruct(line, F32), jax.Sh...  82.1 us
    pallas_call x1, Pallas kernels, per_device(): pl.pallas_call(finish, out_shape=(jax.ShapeDtypeStruct((ROWS,), F32), jax...  3.92 us

profile of v3, /device:TPU:1, one launch (start us, length us, event | category | flops | bytes accessed | tf_op | source)
XLA Modules:
  0.0 86.7 jit_solution(1282163448905853562)
XLA Ops:
  0.6 82.1 %shard_map.128 = (f32[1,384]{1,0:T(1,128)}, bf16[2,128,2048]{2,1,0:T(8,128)(2,1)}, bf16[2,16,2176]{2,1,0:T(8,128)(2,1)}) custom-call(bf16[384,256]{1,0:T(8,128)(2,1)} %feat_hbm.1, f32[384]{0:T(512)} %reward_hbm.1, s32[384]{0:T(512)} %done_hbm.1, f32[384]{0:T(512)} %vnext_hbm.1, f32[384]{0:T(512)} %vnow_hbm.1, bf16[2,256,2048]{2,1,0:T(8,128)(2,1)} %win_hbm.1, ...), custom_call_target="tpu_custom_call" | custom-call | tf_op jit(solution)/shard_map/pallas_call | solution.py:364
  82.7 3.9 %shard_map.129 = (f32[384]{0:T(512)}, f32[16,2,2048]{2,1,0:T(2,128)}, f32[128,2,2048]{2,1,0:T(2,128)}, f32[2,2,128]{2,1,0:T(2,128)}, f32[2,128]{1,0:T(2,128)}) custom-call(f32[1,384]{1,0:T(1,128)} %get-tuple-element.8.vg, bf16[2,128,2048]{2,1,0:T(8,128)(2,1)} %get-tuple-element.9.mid, bf16[2,16,2176]{2,1,0:T(8,128)(2,1)} %get-tuple-element.10.gin), custom_call_target="tpu_custom_call" | custom-call | tf_op jit(solution)/shard_map/pallas_call | solution.py:419

commit v4 on v3

--- a/solution.py
+++ b/solution.py
@@ -343,18 +343,14 @@
 
 
 def finish(vg, mid, gin, vg_out, din, dmid, dbias, dout):
+    vg_out[...] = vg[...].reshape(ROWS)
     for h in range(2):
         dmid[:, h, :] = mid[h].astype(F32)
-
-    @pl.when(pl.program_id(0) == 0)
-    def _():
-        vg_out[...] = vg[...].reshape(ROWS)
-        for h in range(2):
-            din[:, h, :] = gin[h, :, :H].astype(F32)
-            rest = gin[h, :, H:].astype(F32)
-            dbias[0, h : h + 1, :] = rest[0:1]
-            dbias[1, h : h + 1, :] = rest[1:2]
-            dout[h : h + 1, :] = rest[2:3]
+        din[:, h, :] = gin[h, :, :H].astype(F32)
+        rest = gin[h, :, H:].astype(F32)
+        dbias[0, h : h + 1, :] = rest[0:1]
+        dbias[1, h : h + 1, :] = rest[1:2]
+        dout[h : h + 1, :] = rest[2:3]
 
 
 def per_device(features, reward, done, value_next, value_now, w_in, w_mid, biases, w_out):
@@ -425,9 +421,8 @@
             jax.ShapeDtypeStruct((2, 2, 128), F32),
             jax.ShapeDtypeStruct((2, 128), F32),
         ),
-        grid=(4,),
-        in_specs=[vm, pl.BlockSpec((2, 32, H), lambda i: (0, i, 0)), vm],
-        out_specs=(vm, vm, pl.BlockSpec((32, 2, H), lambda i: (i, 0, 0)), vm, vm),
+        in_specs=[vm, vm, vm],
+        out_specs=(vm,) * 5,
     )(vg, mid, gin)
 
 

time: 86.8 us -> 85.8 us (0.988)
  Pallas kernels: 86 us -> 85.1 us
    pallas_call x1, Pallas kernels: 3.92 us -> 3.01 us  [per_device(): pl.pallas_call(finish, out_shape=(jax.ShapeDtypeStruct((ROWS,), F32), jax...]
where the time goes in v4:
time: 85.8 us; the launch traced here: 85.7 us
  Pallas kernels  85.1 us (99%)
    pallas_call x1, Pallas kernels, per_device(): pl.pallas_call(kernel, out_shape=(jax.ShapeDtypeStruct(line, F32), jax.Sh...  82.1 us
    pallas_call x1, Pallas kernels, per_device(): pl.pallas_call(finish, out_shape=(jax.ShapeDtypeStruct((ROWS,), F32), jax...  3.01 us

profile of v4, /device:TPU:1, one launch (start us, length us, event | category | flops | bytes accessed | tf_op | source)
XLA Modules:
  0.0 85.7 jit_solution(1860936119817170978)
XLA Ops:
  0.6 82.1 %shard_map.128 = (f32[1,384]{1,0:T(1,128)}, bf16[2,128,2048]{2,1,0:T(8,128)(2,1)}, bf16[2,16,2176]{2,1,0:T(8,128)(2,1)}) custom-call(bf16[384,256]{1,0:T(8,128)(2,1)} %feat_hbm.1, f32[384]{0:T(512)} %reward_hbm.1, s32[384]{0:T(512)} %done_hbm.1, f32[384]{0:T(512)} %vnext_hbm.1, f32[384]{0:T(512)} %vnow_hbm.1, bf16[2,256,2048]{2,1,0:T(8,128)(2,1)} %win_hbm.1, ...), custom_call_target="tpu_custom_call" | custom-call | tf_op jit(solution)/shard_map/pallas_call | solution.py:360
  82.7 3.0 %shard_map.129 = (f32[384]{0:T(512)}, f32[16,2,2048]{2,1,0:T(2,128)}, f32[128,2,2048]{2,1,0:T(2,128)}, f32[2,2,128]{2,1,0:T(2,128)}, f32[2,128]{1,0:T(2,128)}) custom-call(f32[1,384]{1,0:T(1,128)} %get-tuple-element.8.vg, bf16[2,128,2048]{2,1,0:T(8,128)(2,1)} %get-tuple-element.9.mid, bf16[2,16,2176]{2,1,0:T(8,128)(2,1)} %get-tuple-element.10.gin), custom_call_target="tpu_custom_call" | custom-call | tf_op jit(solution)/shard_map/pallas_call | solution.py:415

commit v5 on v4

--- a/solution.py
+++ b/solution.py
@@ -79,7 +79,7 @@
     for n in range(NC):
         loads.append(
             pltpu.make_async_copy(
-                wmid_hbm.at[head, :, pl.ds(n * C, C)], wmid.at[:, pl.ds(n * C, C)], wsem.at[n]
+                wmid_hbm.at[head, pl.ds(n * C, C)], wmid.at[pl.ds(n * C, C)], wsem.at[n]
             )
         )
     for copy in loads[:2]:

time: 85.8 us -> 85.7 us (level)
  no operation moved by 1% of the time
where the time goes in v5:
time: 85.7 us; the launch traced here: 85.6 us
  Pallas kernels  84.9 us (99%)
    pallas_call x1, Pallas kernels, per_device(): pl.pallas_call(kernel, out_shape=(jax.ShapeDtypeStruct(line, F32), jax.Sh...  81.9 us
    pallas_call x1, Pallas kernels, per_device(): pl.pallas_call(finish, out_shape=(jax.ShapeDtypeStruct((ROWS,), F32), jax...  3.01 us

profile of v5, /device:TPU:1, one launch (start us, length us, event | category | flops | bytes accessed | tf_op | source)
XLA Modules:
  0.0 85.6 jit_solution(9562160748771273570)
XLA Ops:
  0.6 81.9 %shard_map.128 = (f32[1,384]{1,0:T(1,128)}, bf16[2,128,2048]{2,1,0:T(8,128)(2,1)}, bf16[2,16,2176]{2,1,0:T(8,128)(2,1)}) custom-call(bf16[384,256]{1,0:T(8,128)(2,1)} %feat_hbm.1, f32[384]{0:T(512)} %reward_hbm.1, s32[384]{0:T(512)} %done_hbm.1, f32[384]{0:T(512)} %vnext_hbm.1, f32[384]{0:T(512)} %vnow_hbm.1, bf16[2,256,2048]{2,1,0:T(8,128)(2,1)} %win_hbm.1, ...), custom_call_target="tpu_custom_call" | custom-call | tf_op jit(solution)/shard_map/pallas_call | solution.py:360
  82.6 3.0 %shard_map.129 = (f32[384]{0:T(512)}, f32[16,2,2048]{2,1,0:T(2,128)}, f32[128,2,2048]{2,1,0:T(2,128)}, f32[2,2,128]{2,1,0:T(2,128)}, f32[2,128]{1,0:T(2,128)}) custom-call(f32[1,384]{1,0:T(1,128)} %get-tuple-element.8.vg, bf16[2,128,2048]{2,1,0:T(8,128)(2,1)} %get-tuple-element.9.mid, bf16[2,16,2176]{2,1,0:T(8,128)(2,1)} %get-tuple-element.10.gin), custom_call_target="tpu_custom_call" | custom-call | tf_op jit(solution)/shard_map/pallas_call | solution.py:415
